TPU v7x, 256 devices: a 2x2x32 block of a 4x8x32 slice. The times are simulated.
256 devices in a mesh: groups: 4 (over y, x), blk: 32 (over z), span: 2 (over core).
Axes of the slice: x: 2, y: 2, z: 32, core: 2. Of those that a mesh axis runs over, the one named last changes fastest.
The devices are a block of a 4x8x32 slice.
Arguments:
- embeddings: bfloat16 [65536, 768], P(('groups', 'blk', 'span')), parts along dimension 0, may hold values from -6 to 6
- owner_ids: int32 [65536, 1], P(('groups', 'blk', 'span')), parts along dimension 0, may hold values from 0 to 31, as said below
- local_ids: int32 [65536], P(('groups', 'blk', 'span')), parts along dimension 0, may hold values from 0 to 15, as said below
- cluster_map: int32 [2048], P('groups'), parts along dimension 0, may hold values from 0 to 511, as said below
Outputs:
- nearest: float32 [65536], P(('groups', 'blk', 'span')), parts along dimension 0
- centroid_cosine: float32 [65536], P(('groups', 'blk', 'span')), parts along dimension 0
There are 4 independent parts, one for each index of `groups`. A program takes and returns all parts, laid end to end along the dimension named above; each array names one. Nothing has to cross between parts.
Inputs may be any that keep to these rules, and one draw needn't show every extreme that they name: `owner_ids`: at most 16 rows of one device name the same owner; in every draw one owner is named by exactly 16 rows of every device. `local_ids`: of the rows of one device that name one owner, at most 4 have local id 0; in every draw one owner receives exactly 4 rows with local id 0 from every device. In every draw some clusters with a local id other than 0 have exactly one row in the whole shard. cluster_map[o * 16 + l] = o * 16 + l for l > 0. For l = 0 the owners fall into runs of 1 to 3 consecutive owners, and every owner of a run has the value of the run's first owner; some run has 3 owners.
All inputs are finite; a program needn't handle non-finite values.
Results may differ from a plain program's by a relative error of at most 0.0017.
Values may be sent and summed in bfloat16 or wider, within the bound.
A program may use at most 64 MiB of HBM per device.

v0:
```python
import jax
import jax.numpy as jnp
from jax import lax
from jax.sharding import PartitionSpec as P

GIANT_SPAN = 3


def copy_for_each(array, axis):
    copies = jnp.broadcast_to(array, (lax.axis_size(axis), *array.shape))
    return lax.all_to_all(copies, axis, split_axis=0, concat_axis=0, tiled=True)


def in_order(tiles, dim):
    dims = list(tiles.shape[1:])
    dims[dim] *= tiles.shape[0]
    return jnp.moveaxis(tiles, 0, dim).reshape(dims)


def gathered_copies(array, axis, dim):
    tiles = copy_for_each(array, axis)
    return in_order(tiles, dim)


def passed_along(value, axis, steps):
    count = lax.axis_size(axis)
    first, last = (max(0, -steps), min(count, count - steps))
    return lax.ppermute(value, axis, [(source, source + steps) for source in range(first, last)])


def over_copies(array, axis):
    return copy_for_each(array, axis).sum(axis=0)


def in_one_piece(arrays, axis, split_dim, concat_dim, along):
    both = jnp.concatenate(arrays, axis=along)
    whole, at, gathered = (
        lax.all_to_all(both, axis, split_axis=split_dim, concat_axis=concat_dim, tiled=True),
        0,
        [],
    )
    for a in arrays:
        gathered.append(lax.slice_in_dim(whole, at, at + a.shape[along], axis=along))
        at += a.shape[along]
    return tuple(gathered)


def normalize(values):
    wide = values.astype(jnp.float32)
    scale = lax.rsqrt(jnp.sum(wide * wide, axis=1, keepdims=True) + 1e-06)
    return (wide * scale).astype(jnp.bfloat16)


def masked_scores(left, left_tags, right, right_tags):
    scores = lax.dot_general(
        left, right, (((1,), (1,)), ((), ())), preferred_element_type=jnp.float32
    )
    same = (left_tags[:, None] == right_tags[None, :]) & (left_tags[:, None] > 0)
    return jnp.where(same, scores, -1.0)


def body(embeddings, owner_ids, local_ids, cluster_map):
    rows = embeddings.shape[0]
    width = embeddings.shape[1]
    owners = lax.axis_size("blk")
    capacity = 2 * rows // owners
    slots = owners * capacity
    clusters = cluster_map.shape[0]
    owned = clusters // owners
    unit = normalize(embeddings)
    destination = owner_ids[:, 0]
    flat = destination * owned + local_ids
    table = jnp.arange(clusters, dtype=jnp.int32)
    cluster = jnp.sum(jnp.where(flat[:, None] == table[None, :], cluster_map[None, :], 0), axis=1)
    onehot = (destination[:, None] == jnp.arange(owners, dtype=jnp.int32)[None, :]).astype(
        jnp.int32
    )
    before = jnp.cumsum(onehot, axis=0) - onehot
    rank = jnp.sum(before * onehot, axis=1)
    position = destination * capacity + rank
    send_rows = jnp.zeros((slots, width), jnp.bfloat16).at[position].set(unit)
    send_tags = jnp.zeros((slots,), jnp.int32).at[position].set(cluster + 1)
    arrived, arrived_tags = (
        lax.all_to_all(
            send_rows.reshape(owners, capacity, width),
            "blk",
            split_axis=0,
            concat_axis=0,
            tiled=True,
        ),
        lax.all_to_all(
            send_tags.reshape(owners, capacity), "blk", split_axis=0, concat_axis=0, tiled=True
        ),
    )
    mine = arrived.reshape(slots, width)
    my_tags = arrived_tags.reshape(slots)
    chip, chip_tags = (gathered_copies(mine, "span", 0), gathered_copies(my_tags, "span", 0))
    half = lax.axis_index("span")
    block_index = lax.axis_index("blk")
    own_tags = lax.dynamic_slice_in_dim(cluster_map, block_index * owned, owned, 0) + 1
    local = masked_scores(mine, my_tags, chip, chip_tags)
    itself = (
        jnp.arange(2 * slots, dtype=jnp.int32)[None, :]
        == (jnp.arange(slots, dtype=jnp.int32) + half * slots)[:, None]
    )
    best = jnp.max(jnp.where(itself, -1.0, local), axis=1)
    share_limit = 2 * owners * max(1, capacity // 4)
    shared_mask = chip_tags == own_tags[0]
    packed_rank = jnp.cumsum(shared_mask.astype(jnp.int32)) - 1
    target = jnp.where(shared_mask, packed_rank, share_limit)
    packed = jnp.zeros((share_limit, width), jnp.bfloat16).at[target].set(chip, mode="drop")
    packed_tags = jnp.zeros((share_limit,), jnp.int32).at[target].set(chip_tags, mode="drop")
    upper = (packed, packed_tags)
    lower = (packed, packed_tags)
    for step in range(1, GIANT_SPAN):
        upper = passed_along((upper[0], upper[1]), "blk", 1)
        lower = passed_along((lower[0], lower[1]), "blk", -1)
        for other in (upper, lower):
            best = jnp.maximum(
                best, jnp.max(masked_scores(mine, my_tags, other[0], other[1]), axis=1)
            )
    member = my_tags[:, None] == own_tags[None, :]
    local_sums = lax.dot_general(
        member.astype(jnp.bfloat16),
        mine,
        (((0,), (0,)), ((), ())),
        preferred_element_type=jnp.float32,
    )
    chip_sums = over_copies(local_sums, "span")
    totals = chip_sums
    for step in range(1, GIANT_SPAN):
        above = (
            passed_along(chip_sums.astype(jnp.bfloat16), "blk", step).astype(chip_sums.dtype),
            passed_along(own_tags, "blk", step),
        )
        below = (
            passed_along(chip_sums.astype(jnp.bfloat16), "blk", -step).astype(chip_sums.dtype),
            passed_along(own_tags, "blk", -step),
        )
        for other in (above, below):
            match = (own_tags[:, None] == other[1][None, :]).astype(jnp.float32)
            totals = totals + jnp.dot(match, other[0], precision=lax.Precision.HIGHEST)
    length = jnp.sqrt(jnp.sum(totals * totals, axis=1, keepdims=True))
    direction = totals / jnp.maximum(length, 1.0)
    slot_cluster = jnp.sum(
        jnp.where(member, jnp.arange(owned, dtype=jnp.int32)[None, :], 0), axis=1
    )
    slot_cosine = jnp.sum(mine.astype(jnp.float32) * direction[slot_cluster], axis=1)
    returned_best, returned_cosine = in_one_piece(
        (best.reshape(owners, capacity), slot_cosine.reshape(owners, capacity)), "blk", 0, 0, 1
    )
    nearest = returned_best.reshape(slots)[position]
    centroid_cosine = returned_cosine.reshape(slots)[position]
    return (nearest, centroid_cosine)


def solution(mesh):
    return jax.shard_map(
        body,
        mesh=mesh,
        in_specs=(
            P(("groups", "blk", "span"), None),
            P(("groups", "blk", "span"), None),
            P(("groups", "blk", "span")),
            P("groups"),
        ),
        out_specs=(P(("groups", "blk", "span")), P(("groups", "blk", "span"))),
        check_vma=False,
    )
```

profile of v0, /device:TPU:37, one launch (start us, length us, event | category | flops | bytes accessed | tf_op | source)
XLA Modules:
  0.0 257.7 jit_solution(17705456102837070182)
XLA Ops:
  0.6 0.7 multiply_add_fusion
  1.3 0.9 select_reduce_fusion.5
  2.2 0.7 fusion.17
  2.9 0.6 reduce-window.15
  3.7 0.8 fusion.16
  4.5 0.7 compare_select_fusion.3
  5.2 1.4 scatter_custom_fusion
  6.6 0.7 all_to_all.27
  7.3 33.2 %all-to-all-start = ((s32[32,1,16]{2,1,0:T(1,128)}), s32[32,1,16]{2,1,0:T(1,128)S(1)}, u32[]{:S(2)}, u32[]{:S(2)}) async-start(s32[32,1,16]{2,1,0:T(1,128)} %bitcast.5), calls=%async_computation | async-start | bytes 32768 | tf_op jit(solution)/shard_map/all_to_all | solution.py:91
  40.5 1.2 fusion.3
  41.6 3.1 %scatter_custom_fusion.1 = bf16[512,768]{1,0:T(8,128)(2,1)} fusion(s32[256]{0:T(256)S(1)} %bitcast.85, bf16[256,768]{1,0:T(8,128)(2,1)} %param.4, f32[256]{0:T(256)S(1)} %add_rsqrt_fusion, bf16[]{:T(256)} %constant.20.clone.1), kind=kCustom, calls=%fused_computation.24 | custom fusion | flops 589824 | bytes 1180674 | tf_op jit(solution)/shard_map/scatter | solution.py:81
  44.7 16.4 %all-to-all-done = s32[32,1,16]{2,1,0:T(1,128)S(1)} async-done(((s32[32,1,16]{2,1,0:T(1,128)}), s32[32,1,16]{2,1,0:T(1,128)S(1)}, u32[]{:S(2)}, u32[]{:S(2)}) %all-to-all-start) | async-done | bytes 2080 | tf_op jit(solution)/shard_map/all_to_all | solution.py:91
  61.6 0.7 reduce.8
  62.4 5.2 %all_to_all.42 = s32[2,1,512]{2,1,0:T(1,128)S(1)} all-to-all(s32[2,1,512]{2,1,0:T(1,128)S(1)} %broadcast_in_dim.50), channel_id=1, replica_groups=mesh['groups'=4,'blk'=32,'span'=2] {'span'}, dimensions={0} | all-to-all | bytes 8192 | tf_op jit(solution)/shard_map/all_to_all | solution.py:11
  67.6 4.8 %all-to-all-start.2 = ((bf16[32,16,768]{2,1,0:T(8,128)(2,1)}), bf16[32,16,768]{2,1,0:T(8,128)(2,1)S(1)}, u32[]{:S(2)}, u32[]{:S(2)}) async-start(bf16[32,16,768]{2,1,0:T(8,128)(2,1)} %bitcast.7), calls=%async_computation.2 | async-start | bytes 1572864 | tf_op jit(solution)/shard_map/all_to_all | solution.py:84
  72.4 0.8 dynamic-slice_add_fusion
  73.2 1.3 collective-permute-start.14
  74.5 4.9 %collective-permute-start.12 = (s32[16]{0:T(128)S(1)}, s32[16]{0:T(128)S(1)}, u32[]{:S(2)}, u32[]{:S(2)}) collective-permute-start(s32[16]{0:T(128)S(1)} %dynamic-slice_add_fusion), channel_id=1, source_target_pairs={{0,4},{2,6},{4,8},{6,10},{8,12},{10,14},{12,16},{14,18},{16,20},{1... | collective-permute-start | bytes 200 | tf_op jit(solution)/shard_map/ppermute | solution.py:28
  79.5 1.3 collective-permute-start.10
  81.4 4.3 %scatter_custom_fusion.2 = s32[256]{0:T(256)S(1)} fusion(s32[1024]{0:T(1024)S(1)} %bitcast.82, s32[1024]{0:T(1024)S(1)} %bitcast.76, s32[]{:T(128)} %constant.17.clone.1), kind=kCustom, calls=%fused_computation.79 | custom fusion | bytes 1028 | tf_op jit(solution)/shard_map/scatter | solution.py:112
  85.7 1.3 collective-permute-start.2
  87.2 70.8 %all-to-all-done.2 = bf16[32,16,768]{2,1,0:T(8,128)(2,1)S(1)} async-done(((bf16[32,16,768]{2,1,0:T(8,128)(2,1)}), bf16[32,16,768]{2,1,0:T(8,128)(2,1)S(1)}, u32[]{:S(2)}, u32[]{:S(2)}) %all-to-all-start.2) | async-done | bytes 786464 | tf_op jit(solution)/shard_map/all_to_all | solution.py:84
  158.2 5.9 %all_to_all.43 = f32[2,16,768]{2,1,0:T(8,128)S(1)} all-to-all(f32[2,16,768]{2,1,0:T(8,128)S(1)} %broadcast_in_dim.94), channel_id=1, replica_groups=mesh['groups'=4,'blk'=32,'span'=2] {'span'}, dimensions={0} | all-to-all | bytes 196608 | tf_op jit(solution)/shard_map/all_to_all | solution.py:11
  164.1 1.3 collective-permute-start.15
  165.5 5.0 %all_to_all.44 = bf16[2,512,768]{2,1,0:T(8,128)(2,1)S(1)} all-to-all(bf16[2,512,768]{2,1,0:T(8,128)(2,1)S(1)} %broadcast_in_dim.56), channel_id=1, replica_groups=mesh['groups'=4,'blk'=32,'span'=2] {'span'}, dimensions={0} | all-to-all | bytes 3145728 | tf_op jit(solution)/shard_map/all_to_all | solution.py:11
  170.5 1.4 select_reduce_fusion
  171.9 5.2 %scatter_custom_fusion.3 = bf16[256,768]{1,0:T(8,128)(2,1)S(1)} fusion(s32[1024]{0:T(1024)S(1)} %bitcast.83, bf16[1024,768]{1,0:T(8,128)(2,1)S(1)} %bitcast.69, bf16[]{:T(256)} %constant.20.clone.1), kind=kCustom, calls=%fused_computation.27 | custom fusion | bytes 393218 | tf_op jit(solution)/shard_map/scatter | solution.py:111
  177.1 1.3 collective-permute-start
  178.4 5.9 %collective-permute-start.13 = (bf16[16,768]{1,0:T(8,128)(2,1)S(1)}, bf16[16,768]{1,0:T(8,128)(2,1)S(1)}, u32[]{:S(2)}, u32[]{:S(2)}) collective-permute-start(bf16[16,768]{1,0:T(8,128)(2,1)S(1)} %convert_element_type.46), channel_id=1, source_target_pairs={{0,4},{2,6},{4,8},{6,10},{8,12},{10,14},{12,16},{14,18},{16,20},{1... | collective-permute-start | bytes 73736 | tf_op jit(solution)/shard_map/ppermute | solution.py:28
  184.5 1.6 collective-permute-start.8
  186.1 1.3 collective-permute-start.6
  187.4 4.0 %collective-permute-start.4 = (s32[256]{0:T(256)S(1)}, s32[256]{0:T(256)S(1)}, u32[]{:S(2)}, u32[]{:S(2)}) collective-permute-start(s32[256]{0:T(256)S(1)} %collective-permute-done), channel_id=1, source_target_pairs={{0,2},{2,4},{4,6},{6,8},{8,10},{10,12},{12,14},{14,16},{16,18},{18... | collective-permute-start | bytes 3080 | tf_op jit(solution)/shard_map/ppermute | solution.py:28
  191.4 1.3 collective-permute-start.11
  192.9 4.0 %collective-permute-start.9 = (bf16[16,768]{1,0:T(8,128)(2,1)S(1)}, bf16[16,768]{1,0:T(8,128)(2,1)S(1)}, u32[]{:S(2)}, u32[]{:S(2)}) collective-permute-start(bf16[16,768]{1,0:T(8,128)(2,1)S(1)} %convert_element_type.46), channel_id=1, source_target_pairs={{0,2},{2,4},{4,6},{6,8},{8,10},{10,12},{12,14},{14,16},{16,18},{18... | collective-permute-start | bytes 73736 | tf_op jit(solution)/shard_map/ppermute | solution.py:28
  197.0 1.3 collective-permute-start.3
  198.5 4.2 %collective-permute-start.1 = (bf16[256,768]{1,0:T(8,128)(2,1)S(1)}, bf16[256,768]{1,0:T(8,128)(2,1)S(1)}, u32[]{:S(2)}, u32[]{:S(2)}) collective-permute-start(bf16[256,768]{1,0:T(8,128)(2,1)S(1)} %scatter_custom_fusion.3), channel_id=1, source_target_pairs={{0,2},{2,4},{4,6},{6,8},{8,10},{10,12},{12,14},{14,16},{16,18},{18... | collective-permute-start | bytes 1179656 | tf_op jit(solution)/shard_map/ppermute | solution.py:28
  203.1 1.9 gather_fusion
  205.3 2.4 collective-permute-done.3
  207.6 1.3 collective-permute-start.7
  209.0 4.1 %collective-permute-start.5 = (bf16[256,768]{1,0:T(8,128)(2,1)S(1)}, bf16[256,768]{1,0:T(8,128)(2,1)S(1)}, u32[]{:S(2)}, u32[]{:S(2)}) collective-permute-start(bf16[256,768]{1,0:T(8,128)(2,1)S(1)} %collective-permute-done.1), channel_id=1, source_target_pairs={{0,2},{2,4},{4,6},{6,8},{8,10},{10,12},{12,14},{14,16},{16,18},{18... | collective-permute-start | bytes 1179656 | tf_op jit(solution)/shard_map/ppermute | solution.py:28
  213.4 1.4 fusion.42
  214.8 2.7 %collective-permute-done.7 = bf16[256,768]{1,0:T(8,128)(2,1)S(1)} collective-permute-done((bf16[256,768]{1,0:T(8,128)(2,1)}, bf16[256,768]{1,0:T(8,128)(2,1)S(1)}, u32[]{:S(2)}, u32[]{:S(2)}) %collective-permute-start.7) | collective-permute-done | bytes 393248 | tf_op jit(solution)/shard_map/ppermute | solution.py:28
  218.3 0.6 select_reduce_fusion.4
  218.9 0.7 pad_maximum_fusion
  219.6 12.3 %all-to-all-start.5 = ((f32[32,1,32]{2,1,0:T(1,128)}), f32[32,1,32]{2,1,0:T(1,128)S(1)}, u32[]{:S(2)}, u32[]{:S(2)}) async-start(f32[32,1,32]{2,1,0:T(1,128)} %bitcast.19), calls=%async_computation.5 | async-start | bytes 32768 | tf_op jit(solution)/shard_map/all_to_all | solution.py:38
  231.9 20.6 %all-to-all-done.5 = f32[32,1,32]{2,1,0:T(1,128)S(1)} async-done(((f32[32,1,32]{2,1,0:T(1,128)}), f32[32,1,32]{2,1,0:T(1,128)S(1)}, u32[]{:S(2)}, u32[]{:S(2)}) %all-to-all-start.5) | async-done | bytes 4128 | tf_op jit(solution)/shard_map/all_to_all | solution.py:38
  252.7 2.5 gather_fusion.2
  255.2 2.5 gather_fusion.1
  (54 shorter events, 4.6 us)
Async XLA Ops:
  7.3 53.9 %all-to-all-start = ((s32[32,1,16]{2,1,0:T(1,128)}), s32[32,1,16]{2,1,0:T(1,128)S(1)}, u32[]{:S(2)}, u32[]{:S(2)}) async-start(s32[32,1,16]{2,1,0:T(1,128)} %bitcast.5), calls=%async_computation | async-start | bytes 32768 | tf_op jit(solution)/shard_map/all_to_all | solution.py:91
  67.6 90.3 %all-to-all-start.2 = ((bf16[32,16,768]{2,1,0:T(8,128)(2,1)}), bf16[32,16,768]{2,1,0:T(8,128)(2,1)S(1)}, u32[]{:S(2)}, u32[]{:S(2)}) async-start(bf16[32,16,768]{2,1,0:T(8,128)(2,1)} %bitcast.7), calls=%async_computation.2 | async-start | bytes 1572864 | tf_op jit(solution)/shard_map/all_to_all | solution.py:84
  73.2 103.9 %collective-permute-start.14 = (s32[16]{0:T(128)S(1)}, s32[16]{0:T(128)S(1)}, u32[]{:S(2)}, u32[]{:S(2)}) collective-permute-start(s32[16]{0:T(128)S(1)} %dynamic-slice_add_fusion), channel_id=1, source_target_pairs={{4,0},{6,2},{8,4},{10,6},{12,8},{14,10},{16,12},{18,14},{20,16},{2... | collective-permute-start | bytes 200 | tf_op jit(solution)/shard_map/ppermute | solution.py:28
  74.5 109.9 %collective-permute-start.12 = (s32[16]{0:T(128)S(1)}, s32[16]{0:T(128)S(1)}, u32[]{:S(2)}, u32[]{:S(2)}) collective-permute-start(s32[16]{0:T(128)S(1)} %dynamic-slice_add_fusion), channel_id=1, source_target_pairs={{0,4},{2,6},{4,8},{6,10},{8,12},{10,14},{12,16},{14,18},{16,20},{1... | collective-permute-start | bytes 200 | tf_op jit(solution)/shard_map/ppermute | solution.py:28
  79.5 113.5 %collective-permute-start.10 = (s32[16]{0:T(128)S(1)}, s32[16]{0:T(128)S(1)}, u32[]{:S(2)}, u32[]{:S(2)}) collective-permute-start(s32[16]{0:T(128)S(1)} %dynamic-slice_add_fusion), channel_id=1, source_target_pairs={{2,0},{4,2},{6,4},{8,6},{10,8},{12,10},{14,12},{16,14},{18,16},{20... | collective-permute-start | bytes 200 | tf_op jit(solution)/shard_map/ppermute | solution.py:28
  85.7 100.3 %collective-permute-start.2 = (s32[256]{0:T(256)S(1)}, s32[256]{0:T(256)S(1)}, u32[]{:S(2)}, u32[]{:S(2)}) collective-permute-start(s32[256]{0:T(256)S(1)} %scatter_custom_fusion.2), channel_id=1, source_target_pairs={{2,0},{4,2},{6,4},{8,6},{10,8},{12,10},{14,12},{16,14},{18,16},{20... | collective-permute-start | bytes 3080 | tf_op jit(solution)/shard_map/ppermute | solution.py:28
  164.1 14.3 %collective-permute-start.15 = (bf16[16,768]{1,0:T(8,128)(2,1)S(1)}, bf16[16,768]{1,0:T(8,128)(2,1)S(1)}, u32[]{:S(2)}, u32[]{:S(2)}) collective-permute-start(bf16[16,768]{1,0:T(8,128)(2,1)S(1)} %convert_element_type.46), channel_id=1, source_target_pairs={{4,0},{6,2},{8,4},{10,6},{12,8},{14,10},{16,12},{18,14},{20,16},{2... | collective-permute-start | bytes 73736 | tf_op jit(solution)/shard_map/ppermute | solution.py:28
  177.1 10.3 %collective-permute-start = (s32[256]{0:T(256)S(1)}, s32[256]{0:T(256)S(1)}, u32[]{:S(2)}, u32[]{:S(2)}) collective-permute-start(s32[256]{0:T(256)S(1)} %scatter_custom_fusion.2), channel_id=1, source_target_pairs={{0,2},{2,4},{4,6},{6,8},{8,10},{10,12},{12,14},{14,16},{16,18},{18... | collective-permute-start | bytes 3080 | tf_op jit(solution)/shard_map/ppermute | solution.py:28
  178.4 13.0 %collective-permute-start.13 = (bf16[16,768]{1,0:T(8,128)(2,1)S(1)}, bf16[16,768]{1,0:T(8,128)(2,1)S(1)}, u32[]{:S(2)}, u32[]{:S(2)}) collective-permute-start(bf16[16,768]{1,0:T(8,128)(2,1)S(1)} %convert_element_type.46), channel_id=1, source_target_pairs={{0,4},{2,6},{4,8},{6,10},{8,12},{10,14},{12,16},{14,18},{16,20},{1... | collective-permute-start | bytes 73736 | tf_op jit(solution)/shard_map/ppermute | solution.py:28
  184.5 14.0 %collective-permute-start.8 = (s32[16]{0:T(128)S(1)}, s32[16]{0:T(128)S(1)}, u32[]{:S(2)}, u32[]{:S(2)}) collective-permute-start(s32[16]{0:T(128)S(1)} %dynamic-slice_add_fusion), channel_id=1, source_target_pairs={{0,2},{2,4},{4,6},{6,8},{8,10},{10,12},{12,14},{14,16},{16,18},{18... | collective-permute-start | bytes 200 | tf_op jit(solution)/shard_map/ppermute | solution.py:28
  186.1 31.9 %collective-permute-start.6 = (s32[256]{0:T(256)S(1)}, s32[256]{0:T(256)S(1)}, u32[]{:S(2)}, u32[]{:S(2)}) collective-permute-start(s32[256]{0:T(256)S(1)} %collective-permute-done.2), channel_id=1, source_target_pairs={{2,0},{4,2},{6,4},{8,6},{10,8},{12,10},{14,12},{16,14},{18,16},{20... | collective-permute-start | bytes 3080 | tf_op jit(solution)/shard_map/ppermute | solution.py:28
  187.4 30.6 %collective-permute-start.4 = (s32[256]{0:T(256)S(1)}, s32[256]{0:T(256)S(1)}, u32[]{:S(2)}, u32[]{:S(2)}) collective-permute-start(s32[256]{0:T(256)S(1)} %collective-permute-done), channel_id=1, source_target_pairs={{0,2},{2,4},{4,6},{6,8},{8,10},{10,12},{12,14},{14,16},{16,18},{18... | collective-permute-start | bytes 3080 | tf_op jit(solution)/shard_map/ppermute | solution.py:28
  191.4 5.5 %collective-permute-start.11 = (bf16[16,768]{1,0:T(8,128)(2,1)S(1)}, bf16[16,768]{1,0:T(8,128)(2,1)S(1)}, u32[]{:S(2)}, u32[]{:S(2)}) collective-permute-start(bf16[16,768]{1,0:T(8,128)(2,1)S(1)} %convert_element_type.46), channel_id=1, source_target_pairs={{2,0},{4,2},{6,4},{8,6},{10,8},{12,10},{14,12},{16,14},{18,16},{20... | collective-permute-start | bytes 73736 | tf_op jit(solution)/shard_map/ppermute | solution.py:28
  192.9 9.8 %collective-permute-start.9 = (bf16[16,768]{1,0:T(8,128)(2,1)S(1)}, bf16[16,768]{1,0:T(8,128)(2,1)S(1)}, u32[]{:S(2)}, u32[]{:S(2)}) collective-permute-start(bf16[16,768]{1,0:T(8,128)(2,1)S(1)} %convert_element_type.46), channel_id=1, source_target_pairs={{0,2},{2,4},{4,6},{6,8},{8,10},{10,12},{12,14},{14,16},{16,18},{18... | collective-permute-start | bytes 73736 | tf_op jit(solution)/shard_map/ppermute | solution.py:28
  197.0 10.7 %collective-permute-start.3 = (bf16[256,768]{1,0:T(8,128)(2,1)S(1)}, bf16[256,768]{1,0:T(8,128)(2,1)}, u32[]{:S(2)}, u32[]{:S(2)}) collective-permute-start(bf16[256,768]{1,0:T(8,128)(2,1)S(1)} %scatter_custom_fusion.3), channel_id=1, source_target_pairs={{2,0},{4,2},{6,4},{8,6},{10,8},{12,10},{14,12},{16,14},{18,16},{20... | collective-permute-start | bytes 1179656 | tf_op jit(solution)/shard_map/ppermute | solution.py:28
  198.5 10.4 %collective-permute-start.1 = (bf16[256,768]{1,0:T(8,128)(2,1)S(1)}, bf16[256,768]{1,0:T(8,128)(2,1)S(1)}, u32[]{:S(2)}, u32[]{:S(2)}) collective-permute-start(bf16[256,768]{1,0:T(8,128)(2,1)S(1)} %scatter_custom_fusion.3), channel_id=1, source_target_pairs={{0,2},{2,4},{4,6},{6,8},{8,10},{10,12},{12,14},{14,16},{16,18},{18... | collective-permute-start | bytes 1179656 | tf_op jit(solution)/shard_map/ppermute | solution.py:28
  207.6 9.9 %collective-permute-start.7 = (bf16[256,768]{1,0:T(8,128)(2,1)}, bf16[256,768]{1,0:T(8,128)(2,1)S(1)}, u32[]{:S(2)}, u32[]{:S(2)}) collective-permute-start(bf16[256,768]{1,0:T(8,128)(2,1)} %collective-permute-done.3), channel_id=1, source_target_pairs={{2,0},{4,2},{6,4},{8,6},{10,8},{12,10},{14,12},{16,14},{18,16},{20... | collective-permute-start | bytes 1179656 | tf_op jit(solution)/shard_map/ppermute | solution.py:28
  209.0 9.3 %collective-permute-start.5 = (bf16[256,768]{1,0:T(8,128)(2,1)S(1)}, bf16[256,768]{1,0:T(8,128)(2,1)S(1)}, u32[]{:S(2)}, u32[]{:S(2)}) collective-permute-start(bf16[256,768]{1,0:T(8,128)(2,1)S(1)} %collective-permute-done.1), channel_id=1, source_target_pairs={{0,2},{2,4},{4,6},{6,8},{8,10},{10,12},{12,14},{14,16},{16,18},{18... | collective-permute-start | bytes 1179656 | tf_op jit(solution)/shard_map/ppermute | solution.py:28
  219.6 32.9 %all-to-all-start.5 = ((f32[32,1,32]{2,1,0:T(1,128)}), f32[32,1,32]{2,1,0:T(1,128)S(1)}, u32[]{:S(2)}, u32[]{:S(2)}) async-start(f32[32,1,32]{2,1,0:T(1,128)} %bitcast.19), calls=%async_computation.5 | async-start | bytes 32768 | tf_op jit(solution)/shard_map/all_to_all | solution.py:38
where the time goes:
time: 263 us; the launch traced here: 258 us
  waiting for transfers between devices  113 us (43%)
  starting transfers between devices  90.8 us (35%)
  local copies, waits for them, and re-layouts  19.8 us (8%)
  blocking collectives  16.1 us (6%)
  other arithmetic  11.6 us (4%)
  matrix products  5.25 us (2%)
    all_to_all x1, waiting for transfers between devices, body(): lax.all_to_all(send_rows.reshape(owners, capacity, width), 'blk', split_a...  70.8 us
    ppermute x16, starting transfers between devices, passed_along(): lax.ppermute(value, axis, [(source, source + steps) for source in range(f...  40.5 us
    all_to_all x1, starting transfers between devices, body(): lax.all_to_all(send_tags.reshape(owners, capacity), 'blk', split_axis=0,...  33.2 us
    all_to_all x1, waiting for transfers between devices, in_one_piece(): lax.all_to_all(both, axis, split_axis=split_dim, concat_axis=concat_dim,...  20.6 us
    all_to_all x1, waiting for transfers between devices, body(): lax.all_to_all(send_tags.reshape(owners, capacity), 'blk', split_axis=0,...  16.4 us
    all_to_all x3, blocking collectives, copy_for_each(): return lax.all_to_all(copies, axis, split_axis=0, concat_axis=0, tiled=True)  16.1 us
    all_to_all x1, starting transfers between devices, in_one_piece(): lax.all_to_all(both, axis, split_axis=split_dim, concat_axis=concat_dim,...  12.3 us
    ppermute x16, waiting for transfers between devices, passed_along(): lax.ppermute(value, axis, [(source, source + steps) for source in range(f...  5.42 us
  transfers between devices with their start and end apart: 19, of which 6 were waited for; matrix products, arithmetic and copies ran while one was open for 9% of the time, Pallas kernels for 0%

commit v1 on v0

v1 whole, which is shorter than its diff:
```python
import functools

import jax
import jax.numpy as jnp
from jax import lax
from jax.experimental import pallas as pl
from jax.experimental.pallas import tpu as pltpu
from jax.sharding import PartitionSpec as P

MESH = pl.DeviceIdType.MESH
LANES = 128
F32 = jnp.float32
BF16 = jnp.bfloat16


def dot(left, right, dims, precision=None):
    return lax.dot_general(
        left, right, (dims, ((), ())), preferred_element_type=F32, precision=precision
    )


def iota(shape, dim):
    return lax.broadcasted_iota(jnp.int32, shape, dim)


def column(row):
    eye = iota((LANES, LANES), 0) == iota((LANES, LANES), 1)
    pieces = []
    for at in range(0, row.shape[1], LANES):
        piece = jnp.where(eye, row[:, at : at + LANES], 0.0)
        pieces.append(jnp.sum(piece, axis=1, keepdims=True))
    return jnp.concatenate(pieces, axis=0)


def farthest_first(j, owners):
    return owners // 2 + (1 - 2 * lax.rem(j, 2)) * ((j + 1) // 2)


def kernel(
    owners,
    capacity,
    shared,
    owned,
    emb_hbm,
    owner_hbm,
    local_hbm,
    map_hbm,
    near_ref,
    cos_ref,
    emb,
    owner_row,
    local_row,
    map_row,
    place,
    packed,
    tags_out,
    mine,
    peer,
    tags_in,
    tags_mine,
    tags_peer,
    giant,
    giant_tags,
    side,
    side_peer,
    side_tags,
    side_tags_peer,
    mid_out,
    mid_in,
    reply_out,
    reply_in,
    in_sem,
    row_send,
    row_recv,
    tag_send,
    tag_recv,
    peer_send,
    peer_recv,
    ptag_send,
    ptag_recv,
    side_send,
    side_recv,
    stag_send,
    stag_recv,
    spx_send,
    spx_recv,
    spt_send,
    spt_recv,
    mid_send,
    mid_recv,
    reply_send,
    reply_recv,
):
    me = lax.axis_index("blk")
    half = lax.axis_index("span")
    rows, width = emb_hbm.shape
    slots = owners * capacity
    per_chunk = LANES // capacity
    chunks = slots // LANES
    many = owners * shared

    def at(step):
        return {"blk": lax.rem(me + step, owners), "span": half}

    other = {"blk": me, "span": 1 - half}

    barrier = pltpu.get_barrier_semaphore()

    def greet(j, carry):
        step = farthest_first(j, owners)
        pl.semaphore_signal(barrier, inc=1, device_id=at(step), device_id_type=MESH)
        return carry

    loads = [
        pltpu.make_async_copy(source, target, in_sem.at[i])
        for i, (source, target) in enumerate(
            (
                (emb_hbm, emb),
                (owner_hbm, owner_row),
                (local_hbm, local_row),
                (map_hbm, map_row),
            )
        )
    ]
    for load in loads:
        load.start()
    lax.fori_loop(0, owners - 1, greet, 0)
    pl.semaphore_signal(barrier, inc=1, device_id=other, device_id_type=MESH)
    for load in loads:
        load.wait()

    relative = owner_row[...] - me
    relative = jnp.where(relative < 0, relative + owners, relative)
    local = local_row[...]
    to_owner = relative == iota((owners, rows), 0)
    first = local == 0
    one_first = jnp.where(to_owner & first, 1.0, 0.0)
    one_rest = jnp.where(to_owner & ~first, 1.0, 0.0)
    before = jnp.where(iota((rows, rows), 0) < iota((rows, rows), 1), 1.0, 0.0).astype(BF16)
    both = jnp.concatenate([one_first, one_rest], axis=0).astype(BF16)
    prefix = dot(both, before, ((1,), (0,)))
    heads = jnp.sum(one_first, axis=1, keepdims=True)
    rank = jnp.sum(
        one_first * prefix[:owners] + one_rest * (prefix[owners:] + heads), axis=0, keepdims=True
    )
    position = relative.astype(F32) * capacity + rank
    placed = jnp.where(iota((slots, rows), 0).astype(F32) == position, 1.0, 0.0).astype(BF16)
    place[...] = placed

    wide = emb[...].astype(F32)
    scale = lax.rsqrt(jnp.sum(wide * wide, axis=1, keepdims=True) + 1e-06)
    unit = (wide * scale).astype(BF16)
    packed[...] = (
        dot(placed, unit, ((1,), (0,))).astype(BF16).reshape(owners, capacity, width)
    )
    tag_lhs = jnp.broadcast_to((local + 1).astype(F32), (8, rows)).astype(BF16)
    tag_row = dot(tag_lhs, placed, ((1,), (1,)))[:1]
    for c in range(chunks):
        tags_out[c] = tag_row[:, c * LANES : (c + 1) * LANES]
    mine[0] = packed[0]
    tags_in[0] = tags_out[0]

    pl.semaphore_wait(barrier, owners)

    def send_rows(step):
        return pltpu.make_async_remote_copy(
            src_ref=packed.at[step],
            dst_ref=mine.at[step],
            send_sem=row_send.at[step],
            recv_sem=row_recv.at[step],
            device_id=at(step),
            device_id_type=MESH,
        )

    def send_tags(step):
        return pltpu.make_async_remote_copy(
            src_ref=tags_out.at[step // per_chunk],
            dst_ref=tags_in.at[step],
            send_sem=tag_send.at[step],
            recv_sem=tag_recv.at[step],
            device_id=at(step),
            device_id_type=MESH,
        )

    def to_peer(source, step):
        return pltpu.make_async_remote_copy(
            src_ref=source.at[step],
            dst_ref=peer.at[step],
            send_sem=peer_send.at[step],
            recv_sem=peer_recv.at[step],
            device_id=other,
            device_id_type=MESH,
        )

    def start_rows(j, carry):
        step = farthest_first(j, owners)
        send_tags(step).start()
        send_rows(step).start()
        return carry

    lax.fori_loop(0, owners - 1, start_rows, 0)
    to_peer(packed, 0).start()

    def take_rows(j, carry):
        step = farthest_first(j, owners)
        send_tags(step).wait_recv()
        send_rows(step).wait_recv()
        to_peer(mine, step).start()
        return carry

    lax.fori_loop(0, owners - 1, take_rows, 0)

    lane_group = iota((1, LANES), 1) // capacity
    row_parts = []
    for c in range(chunks):
        part = jnp.zeros((1, LANES), F32)
        for g in range(per_chunk):
            part = jnp.where(lane_group == g, tags_in[c * per_chunk + g], part)
        tags_mine[c] = part
        row_parts.append(part)
    my_tags = jnp.concatenate(row_parts, axis=1)
    peer_tags_copy = pltpu.make_async_remote_copy(
        src_ref=tags_mine,
        dst_ref=tags_peer,
        send_sem=ptag_send,
        recv_sem=ptag_recv,
        device_id=other,
        device_id_type=MESH,
    )
    peer_tags_copy.start()

    own_rows = mine[...].reshape(slots, width)
    slot_of = capacity * (iota((many, slots), 0) // shared) + lax.rem(
        iota((many, slots), 0), shared
    )
    picked = slot_of == iota((many, slots), 1)
    giant[...] = dot(jnp.where(picked, 1.0, 0.0).astype(BF16), own_rows, ((1,), (0,))).astype(
        BF16
    )
    my_column = column(my_tags)
    slot_back = capacity * (iota((slots, many), 1) // shared) + lax.rem(
        iota((slots, many), 1), shared
    )
    picked_back = slot_back == iota((slots, many), 0)
    giant_tags[0] = jnp.sum(
        jnp.where(picked_back & (my_column == 1.0), 1.0, 0.0), axis=0, keepdims=True
    )

    def to_side(which):
        step = 1 if which == 0 else owners - 1
        return (
            pltpu.make_async_remote_copy(
                src_ref=giant,
                dst_ref=side.at[which],
                send_sem=side_send.at[which],
                recv_sem=side_recv.at[which],
                device_id=at(step),
                device_id_type=MESH,
            ),
            pltpu.make_async_remote_copy(
                src_ref=giant_tags.at[0],
                dst_ref=side_tags.at[which],
                send_sem=stag_send.at[which],
                recv_sem=stag_recv.at[which],
                device_id=at(step),
                device_id_type=MESH,
            ),
        )

    sides = [to_side(0), to_side(1)]
    for copies in sides:
        for copy in copies:
            copy.start()

    best = jnp.full((1, slots), -1.0, F32)
    block = 256
    for at_row in range(0, slots, block):
        part = own_rows[at_row : at_row + block]
        scores = dot(part, own_rows, ((1,), (1,)))
        same = my_column[at_row : at_row + block] == my_tags
        itself = (iota((block, slots), 0) + at_row) == iota((block, slots), 1)
        scores = jnp.where(same & ~itself, scores, -1.0)
        best = jnp.maximum(best, jnp.max(scores, axis=0, keepdims=True))

    peer_tags_copy.wait_recv()
    for step in range(owners):
        to_peer(packed if step == 0 else mine, step).wait_recv()
    peer_row = jnp.concatenate([tags_peer[c] for c in range(chunks)], axis=1)
    peer_column = column(peer_row)
    peer_rows = peer[...].reshape(slots, width)
    for at_row in range(0, slots, block):
        part = peer_rows[at_row : at_row + block]
        scores = dot(part, own_rows, ((1,), (1,)))
        same = peer_column[at_row : at_row + block] == my_tags
        scores = jnp.where(same, scores, -1.0)
        best = jnp.maximum(best, jnp.max(scores, axis=0, keepdims=True))
    ids = (iota((owned, slots), 0) + 1).astype(F32)
    sums = dot(jnp.where(ids == my_tags, 1.0, 0.0).astype(BF16), own_rows, ((1,), (0,)))
    sums += dot(jnp.where(ids == peer_row, 1.0, 0.0).astype(BF16), peer_rows, ((1,), (0,)))

    def side_to_peer(which):
        return (
            pltpu.make_async_remote_copy(
                src_ref=side.at[which],
                dst_ref=side_peer.at[which],
                send_sem=spx_send.at[which],
                recv_sem=spx_recv.at[which],
                device_id=other,
                device_id_type=MESH,
            ),
            pltpu.make_async_remote_copy(
                src_ref=side_tags.at[which],
                dst_ref=side_tags_peer.at[which],
                send_sem=spt_send.at[which],
                recv_sem=spt_recv.at[which],
                device_id=other,
                device_id_type=MESH,
            ),
        )

    shares = [side_to_peer(0), side_to_peer(1)]
    for copies, share in zip(sides, shares):
        for copy, on in zip(copies, share):
            copy.wait_recv()
            on.start()
    for share in shares:
        for on in share:
            on.wait_recv()

    lane = iota(map_row.shape, 1)

    def number(step):
        owner = lax.rem(me + step, owners)
        return jnp.sum(
            jnp.where(lane == owner * owned, map_row[...], 0), axis=1, keepdims=True
        )

    here, up, down = number(0), number(1), number(owners - 1)
    near = [jnp.where(here == down, 1.0, 0.0), jnp.where(here == up, 1.0, 0.0)]
    across = jnp.where(up == down, 1.0, 0.0)

    rows_of = [jnp.concatenate([side[w], side_peer[w]], axis=0) for w in (0, 1)]
    tags_of = [jnp.concatenate([side_tags[w], side_tags_peer[w]], axis=1) for w in (0, 1)]
    columns_of = [column(t) for t in tags_of]
    side_sums = [
        dot(jnp.broadcast_to(tags_of[w], (8, 2 * many)).astype(BF16), rows_of[w], ((1,), (0,)))[:1]
        for w in (0, 1)
    ]
    for w in (0, 1):
        far = 1 - w
        scores = dot(rows_of[far], side[w], ((1,), (1,)))
        keep = (columns_of[far] * across) > 0.5
        top = jnp.max(jnp.where(keep, scores, -1.0), axis=0, keepdims=True)
        mid_out[w, :, :LANES] = top
        mid_out[w, :, LANES:] = side_sums[far] * across

    def to_mid(w):
        return pltpu.make_async_remote_copy(
            src_ref=mid_out.at[w],
            dst_ref=mid_in.at[1 - w],
            send_sem=mid_send.at[w],
            recv_sem=mid_recv.at[1 - w],
            device_id=at(owners - 1 if w == 0 else 1),
            device_id_type=MESH,
        )

    def from_mid(w):
        return pltpu.make_async_remote_copy(
            src_ref=mid_out.at[w],
            dst_ref=mid_in.at[w],
            send_sem=mid_send.at[w],
            recv_sem=mid_recv.at[w],
            device_id=at(owners - 1 if w == 0 else 1),
            device_id_type=MESH,
        )

    for w in (0, 1):
        to_mid(w).start()

    shared_here = my_tags == 1.0
    for w in (0, 1):
        scores = dot(rows_of[w], own_rows, ((1,), (1,)))
        keep = ((columns_of[w] * near[w]) > 0.5) & shared_here
        best = jnp.maximum(
            best, jnp.max(jnp.where(keep, scores, -1.0), axis=0, keepdims=True)
        )
    extra = side_sums[0] * near[0] + side_sums[1] * near[1]

    for w in (0, 1):
        from_mid(w).wait_recv()
    top = jnp.maximum(mid_in[0, :, :LANES], mid_in[1, :, :LANES])
    spread = jnp.max(jnp.where(picked, column(top), -1.0), axis=0, keepdims=True)
    best = jnp.maximum(best, jnp.where(shared_here, spread, -1.0))
    extra += mid_in[0, :, LANES:] + mid_in[1, :, LANES:]
    sums += jnp.where(iota((owned, width), 0) == 0, extra, 0.0)

    length = jnp.sqrt(jnp.sum(sums * sums, axis=1, keepdims=True))
    direction = sums / jnp.maximum(length, 1.0)
    high = direction.astype(BF16)
    low = (direction - high.astype(F32)).astype(BF16)
    cosines = dot(jnp.concatenate([high, low], axis=0), own_rows, ((1,), (1,)))
    cosines = cosines[:owned] + cosines[owned:]
    cosine = jnp.sum(jnp.where(ids == my_tags, cosines, 0.0), axis=0, keepdims=True)

    for c in range(chunks):
        reply_out[c, 0:1] = best[:, c * LANES : (c + 1) * LANES]
        reply_out[c, 1:2] = cosine[:, c * LANES : (c + 1) * LANES]

    def send_reply(step):
        return pltpu.make_async_remote_copy(
            src_ref=reply_out.at[step // per_chunk],
            dst_ref=reply_in.at[step],
            send_sem=reply_send.at[step],
            recv_sem=reply_recv.at[step],
            device_id=at(owners - step),
            device_id_type=MESH,
        )

    def start_reply(j, carry):
        send_reply(farthest_first(j, owners)).start()
        return carry

    lax.fori_loop(0, owners - 1, start_reply, 0)
    reply_in[0] = reply_out[0]

    def drain(j, carry):
        step = farthest_first(j, owners)
        send_rows(step).wait_send()
        send_tags(step).wait_send()
        to_peer(mine, step).wait_send()
        return carry

    lax.fori_loop(0, owners - 1, drain, 0)
    to_peer(packed, 0).wait_send()
    peer_tags_copy.wait_send()
    for copies in sides + shares:
        for copy in copies:
            copy.wait_send()
    for w in (0, 1):
        to_mid(w).wait_send()

    def take_reply(j, carry):
        step = owners - 1 - j
        send_reply(step).wait()
        return carry

    lax.fori_loop(0, owners - 1, take_reply, 0)

    parts = []
    for c in range(chunks):
        part = jnp.zeros((2, LANES), F32)
        for g in range(per_chunk):
            part = jnp.where(lane_group == g, reply_in[c * per_chunk + g], part)
        parts.append(part)
    values = jnp.concatenate(parts, axis=1)
    one = values.astype(BF16)
    rest = values - one.astype(F32)
    two = rest.astype(BF16)
    three = (rest - two.astype(F32)).astype(BF16)
    chosen = dot(jnp.concatenate([one, two, three], axis=0), place[...], ((1,), (0,)))
    result = chosen[0:2] + chosen[2:4] + chosen[4:6]
    near_ref[...] = result[0:1]
    cos_ref[...] = result[1:2]


def body(embeddings, owner_ids, local_ids, cluster_map):
    rows, width = embeddings.shape
    owners = lax.axis_size("blk")
    capacity = 2 * rows // owners
    shared = max(1, capacity // 4)
    slots = owners * capacity
    clusters = cluster_map.shape[0]
    owned = clusters // owners
    chunks = slots // LANES
    many = owners * shared
    dma = pltpu.SemaphoreType.DMA
    vmem = pltpu.VMEM
    near, cosine = pl.pallas_call(
        functools.partial(kernel, owners, capacity, shared, owned),
        out_shape=[jax.ShapeDtypeStruct((1, rows), F32)] * 2,
        in_specs=[pl.BlockSpec(memory_space=pl.ANY)] * 4,
        out_specs=[pl.BlockSpec(memory_space=pltpu.VMEM)] * 2,
        scratch_shapes=[
            vmem((rows, width), BF16),
            vmem((1, rows), jnp.int32),
            vmem((1, rows), jnp.int32),
            vmem((1, clusters), jnp.int32),
            vmem((slots, rows), BF16),
            vmem((owners, capacity, width), BF16),
            vmem((chunks, 1, LANES), F32),
            vmem((owners, capacity, width), BF16),
            vmem((owners, capacity, width), BF16),
            vmem((owners, 1, LANES), F32),
            vmem((chunks, 1, LANES), F32),
            vmem((chunks, 1, LANES), F32),
            vmem((many, width), BF16),
            vmem((1, 1, LANES), F32),
            vmem((2, many, width), BF16),
            vmem((2, many, width), BF16),
            vmem((2, 1, LANES), F32),
            vmem((2, 1, LANES), F32),
            vmem((2, 1, LANES + width), F32),
            vmem((2, 1, LANES + width), F32),
            vmem((chunks, 2, LANES), F32),
            vmem((owners, 2, LANES), F32),
            dma((4,)),
            dma((owners,)),
            dma((owners,)),
            dma((owners,)),
            dma((owners,)),
            dma((owners,)),
            dma((owners,)),
            dma,
            dma,
            dma((2,)),
            dma((2,)),
            dma((2,)),
            dma((2,)),
            dma((2,)),
            dma((2,)),
            dma((2,)),
            dma((2,)),
            dma((2,)),
            dma((2,)),
            dma((owners,)),
            dma((owners,)),
        ],
        compiler_params=pltpu.CompilerParams(collective_id=0, has_side_effects=True),
    )(
        embeddings,
        owner_ids.reshape(1, rows),
        local_ids.reshape(1, rows),
        cluster_map.reshape(1, clusters),
    )
    return near.reshape(rows), cosine.reshape(rows)


def solution(mesh):
    return jax.shard_map(
        body,
        mesh=mesh,
        in_specs=(
            P(("groups", "blk", "span"), None),
            P(("groups", "blk", "span"), None),
            P(("groups", "blk", "span")),
            P("groups"),
        ),
        out_specs=(P(("groups", "blk", "span")), P(("groups", "blk", "span"))),
        check_vma=False,
    )
```

time: 263 us -> 133 us (0.51); the launches traced: 258 us -> 133 us
  Pallas kernels: 0 us -> 131 us
  waiting for transfers between devices: 113 us -> 0 us
  starting transfers between devices: 90.8 us -> 0 us
  local copies, waits for them, and re-layouts: 19.8 us -> 1.86 us
  blocking collectives: 16.1 us -> 0 us
  other arithmetic: 11.6 us -> 0 us
  matrix products: 5.25 us -> 0 us
    pallas_call x0 -> x1, Pallas kernels: none -> 131 us  [body(): pl.pallas_call(functools.partial(kernel, owners, capacity, shared, owned)...]
    all_to_all x3 -> x0, waiting for transfers between devices: 108 us -> none  [the longest x1 70.8 us: body(): lax.all_to_all(send_rows.reshape(owners, capacity, width), 'blk', split_a...]
    all_to_all x3 -> x0, starting transfers between devices: 50.3 us -> none  [the longest x1 33.2 us: body(): lax.all_to_all(send_tags.reshape(owners, capacity), 'blk', split_axis=0,...]
    ppermute x16 -> x0, starting transfers between devices: 40.5 us -> none  [passed_along(): lax.ppermute(value, axis, [(source, source + steps) for source in range(f...]
    all_to_all x3 -> x0, blocking collectives: 16.1 us -> none  [copy_for_each(): return lax.all_to_all(copies, axis, split_axis=0, concat_axis=0, tiled=True)]
    scatter x3 -> x0, local copies, waits for them, and re-layouts: 10.9 us -> none  [the longest x1 5.16 us: body(): jnp.zeros((share_limit, width), jnp.bfloat16).at[target]]
    gather x3 -> x0, local copies, waits for them, and re-layouts: 6.9 us -> none  [the longest x1 2.51 us: body(): centroid_cosine = returned_cosine.reshape(slots)[position]]
    ppermute x16 -> x0, waiting for transfers between devices: 5.42 us -> none  [passed_along(): lax.ppermute(value, axis, [(source, source + steps) for source in range(f...]
  transfers between devices with their start and end apart: 19 -> 0, of which waited for: 6 -> 0; matrix products, arithmetic and copies ran while one was open for 9% -> 0% of each run, Pallas kernels for 0% -> 0%
where the time goes in v1:
time: 133 us
  Pallas kernels  131 us (98%)
  local copies, waits for them, and re-layouts  1.86 us (1%)
    pallas_call x1, Pallas kernels, body(): pl.pallas_call(functools.partial(kernel, owners, capacity, shared, owned)...  131 us

profile of v1, /device:TPU:37, one launch (start us, length us, event | category | flops | bytes accessed | tf_op | source)
XLA Modules:
  0.0 133.2 jit_solution(10989191140084264719)
XLA Ops:
  0.6 130.7 %shard_map.59 = (f32[1,256]{1,0:T(1,128)}, f32[1,256]{1,0:T(1,128)}) custom-call(bf16[256,768]{1,0:T(8,128)(2,1)} %emb_hbm.1, s32[1,256]{1,0:T(1,128)} %bitcast.6, s32[1,256]{1,0:T(1,128)} %bitcast.7, s32[1,512]{1,0:T(1,128)} %bitcast.5), custom_call_target="tpu_custom_call" | custom-call | tf_op jit(solution)/shard_map/pallas_call | solution.py:478
  131.3 0.0 copy-start.1
  131.3 0.7 copy-done.1
  132.0 0.0 copy-start
  132.0 0.6 copy.8
  132.6 0.1 copy-done
  132.6 0.6 copy.9
Async XLA Ops:
  131.3 0.7 copy-start.1
  132.0 0.6 copy-start
